TPU v7x, 32 devices: a whole 2x2x4 slice. The times are simulated.
32 devices in a mesh: lat: 16 (over z, x, core), tm: 2 (over y).
Axes of the slice: x: 2, y: 2, z: 4, core: 2. Of those that a mesh axis runs over, the one named last changes fastest.
Arguments:
- fields: bfloat16 [512, 64, 1024], P('lat', 'tm'), may hold values from -16 to 16
Outputs:
- covariance: float32 [64, 64], P('tm')
All inputs are finite; a program needn't handle non-finite values.
Results may differ from a plain program's by a relative error of at most 0.0003.
Values may be sent and summed in bfloat16 or wider, within the bound.
A program may use at most 64 MiB of HBM per device.

v0:
```python
import math
import jax
import jax.numpy as jnp
from jax import lax
from jax.sharding import PartitionSpec as P

TRUNC = 341
MSLOT = 384
DSLOT = 384


def start_value(order, sine_lat):
    log_start = 0.5 * (
        math.log(0.5)
        + lax.lgamma(order + 1.5)
        - (0.5 * math.log(math.pi) - math.log(2.0))
        - lax.lgamma(order + 1.0)
    ) + order * jnp.log(sine_lat)
    taper = jnp.clip((log_start + 70.0) / 10.0, 0.0, 1.0)
    return jnp.exp(jnp.maximum(log_start, -80.0)) * taper


def step_factors(order, degree):
    top = jnp.sqrt((4.0 * degree * degree - 1.0) / (degree * degree - order * order))
    below = degree - 1.0
    back = jnp.sqrt(
        jnp.maximum(below * below - order * order, 0.0) / jnp.abs(4.0 * below * below - 1.0)
    )
    return (top, top * back)


def legendre_blocks(orders, cosine_lat, sine_lat):
    order_total = orders.shape[0]
    lat_total = cosine_lat.shape[0]
    block_total = 16
    block_length = DSLOT // block_total
    order_grid = orders[:, None, None]
    cosine_grid = cosine_lat[None, :, None]
    block_base = (jnp.arange(block_total) * block_length).astype(jnp.float32)[None, None, :]
    unit = jnp.ones((order_total, lat_total, block_total), jnp.float32)
    empty = jnp.zeros_like(unit)

    def compose(position, matrices):
        upper_left, upper_right, lower_left, lower_right = matrices
        top, mixed = step_factors(
            order_grid, order_grid + block_base + position.astype(jnp.float32)
        )
        diagonal_term = top * cosine_grid
        return (
            diagonal_term * upper_left - mixed * lower_left,
            diagonal_term * upper_right - mixed * lower_right,
            upper_left,
            upper_right,
        )

    upper_left, upper_right, lower_left, lower_right = lax.fori_loop(
        1, block_length + 1, compose, (unit, empty, empty, unit)
    )
    current = start_value(orders[:, None], sine_lat[None, :])
    previous = jnp.zeros_like(current)
    current_list = []
    previous_list = []
    for block in range(block_total):
        current_list.append(current)
        previous_list.append(previous)
        current, previous = (
            upper_left[:, :, block] * current + upper_right[:, :, block] * previous,
            lower_left[:, :, block] * current + lower_right[:, :, block] * previous,
        )
    current = jnp.stack(current_list, axis=-1)
    previous = jnp.stack(previous_list, axis=-1)
    outputs = []
    for position in range(1, block_length + 1):
        outputs.append(current)
        top, mixed = step_factors(order_grid, order_grid + block_base + float(position))
        current, previous = (top * cosine_grid * current - mixed * previous, current)
    values = jnp.stack(outputs, axis=-1)
    return values.reshape(order_total, lat_total, DSLOT)


def weighted_basis(orders, cosine_lat, sine_lat, weight):
    values = legendre_blocks(orders, cosine_lat, sine_lat)
    offsets = jnp.arange(DSLOT).astype(jnp.float32)
    keep = (orders[:, None] + offsets[None, :] <= TRUNC).astype(jnp.float32)
    factor = jnp.where(orders > 0, math.sqrt(2.0), 1.0)
    table = values * keep[:, None, :] * weight[None, :, None] * factor[:, None, None]
    return table.astype(jnp.bfloat16)


def local(fields):
    row_count, month_count, lon_count = fields.shape
    lat_devices = lax.axis_size("lat")
    slots_dev = MSLOT // lat_devices
    lat_index = lax.axis_index("lat")
    column = jnp.arange(2 * MSLOT)
    group = column // (2 * slots_dev)
    inner = column % (2 * slots_dev) // 2
    part_index = column % 2
    own_inner = jnp.arange(slots_dev)
    wave_order = group * slots_dev + inner
    own_order = lat_index * slots_dev + own_inner
    longitude = jnp.arange(lon_count)
    phase = (
        2.0
        * math.pi
        * (wave_order[:, None] * longitude[None, :] % lon_count).astype(jnp.float32)
        / lon_count
    )
    active = (wave_order <= TRUNC).astype(jnp.float32)[:, None]
    transform = (
        jnp.where(part_index[:, None] == 0, jnp.cos(phase), -jnp.sin(phase))
        * active
        / math.sqrt(lon_count)
    )
    transform = transform.astype(jnp.bfloat16)
    flat_fields = fields.reshape(row_count * month_count, lon_count)
    fourier = lax.dot_general(
        transform, flat_fields, (((1,), (1,)), ((), ())), preferred_element_type=jnp.float32
    )
    fourier = fourier.astype(jnp.bfloat16).reshape(2 * MSLOT, row_count, month_count)
    moved = lax.all_to_all(fourier, "lat", split_axis=0, concat_axis=1, tiled=True)
    lat_count = moved.shape[1]
    theta = math.pi * (jnp.arange(lat_count).astype(jnp.float32) + 0.5) / lat_count
    cosine_lat = jnp.cos(theta)
    sine_lat = jnp.sin(theta)
    weight = math.pi * sine_lat / lat_count
    basis = weighted_basis(own_order.astype(jnp.float32), cosine_lat, sine_lat, weight)
    moved_data = moved.reshape(slots_dev, 2, lat_count, month_count)
    coefficients = jnp.einsum(
        "srjt,sjd->tsrd", moved_data, basis, preferred_element_type=jnp.float32
    )
    coefficients = coefficients.astype(jnp.bfloat16).reshape(month_count, -1)
    tm_devices = lax.axis_size("tm")
    total_months = month_count * tm_devices
    columns = lax.all_to_all(coefficients, "tm", split_axis=1, concat_axis=0, tiled=True)
    partial_gram = lax.psum_scatter(
        lax.dot_general(
            columns, columns, (((1,), (1,)), ((), ())), preferred_element_type=jnp.float32
        ),
        "tm",
        scatter_dimension=0,
        tiled=True,
    )
    gram = lax.psum(partial_gram, "lat")
    own_block = lax.dynamic_slice_in_dim(gram, lax.axis_index("tm") * month_count, month_count, 1)
    trace_total = lax.psum(jnp.sum(jnp.diagonal(own_block)), "tm")
    return total_months * gram / (trace_total + 1e-06)


def solution(mesh):
    placed = (P("lat", "tm", None),)
    return jax.shard_map(
        local, mesh=mesh, in_specs=placed, out_specs=P("tm", None), check_vma=False
    )
```

profile of v0, /device:TPU:0, one launch (start us, length us, event | category | flops | bytes accessed | tf_op | source)
XLA Modules:
  0.0 353.8 jit_solution(13318265986543368269)
XLA Ops:
  6.6 1.5 copy-done
  8.1 16.4 %convolution_convert_fusion = bf16[768,1024]{1,0:T(8,128)(2,1)} fusion(bf16[1024,1024]{1,0:T(8,128)(2,1)S(1)} %bitcast.84, f32[768]{0:T(1024)S(1)} %get-tuple-element.432, s32[768]{0:T(1024)S(1)} %fusion.324, pred[768]{0:T(1024)(128)(4,1)S(1)} %get-tuple-element.431), kind=kOutput, calls=%fused_computation.41 | convolution fusion | flops 1626341376 | bytes 3676928 | tf_op jit(solution)/shard_map/dot_general | solution.py:117
  24.5 1.7 copy.127
  26.2 9.2 %copy.128 = bf16[768,32,32]{2,1,0:T(8,128)(2,1)} copy(bf16[768,32,32]{0,2,1:T(8,128)(2,1)S(1)} %bitcast.90) | data formatting | bytes 3145728 | tf_op jit(solution)/shard_map/reshape | solution.py:120
  35.4 9.3 %reshape.8823 = bf16[16,2,24576]{2,1,0:T(2,128)(2,1)} reshape(bf16[768,32,32]{2,1,0:T(8,128)(2,1)} %copy.128) | data formatting | bytes 3145728
  44.7 7.4 %all-to-all-start = ((bf16[16,2,24576]{2,1,0:T(2,128)(2,1)}), bf16[16,2,24576]{2,1,0:T(2,128)(2,1)}, u32[]{:S(2)}, u32[]{:S(2)}) async-start(bf16[16,2,24576]{2,1,0:T(2,128)(2,1)} %reshape.8823), calls=%async_computation | async-start | bytes 3145728 | tf_op jit(solution)/shard_map/all_to_all | solution.py:121
  53.3 71.6 %while.25 = (s32[]{:T(128)}, f32[24,512,16]{1,2,0:T(8,128)S(1)}, f32[24,512,16]{1,2,0:T(8,128)}, f32[24,512,16]{1,2,0:T(8,128)S(1)}, f32[24,512,16]{1,2,0:T(8,128)S(1)}, /*index=5*/s32[]{:T(128)}, s32[]{:T(128)}, s32[]{:T(128)}) while((s32[]{:T(128)}, f32[24,512,16]{1,2,0:T(8,128)S(1)}, ...), condition=%wide.region_1.2_spmd.clone.clone.clone, body=%wide.region_0.1_spmd.clone.clone.clone.sunk | while | flops 1778076 | bytes 6308475 | solution.py:56
  53.6 1.5 fusion.362
  55.5 2.7 fusion.362
  58.6 2.7 fusion.362
  61.6 2.7 fusion.362
  64.6 2.7 fusion.362
  67.6 2.7 fusion.362
  70.7 2.7 fusion.362
  73.7 2.7 fusion.362
  76.7 2.7 fusion.362
  79.8 2.7 fusion.362
  82.8 2.7 fusion.362
  85.8 2.7 fusion.362
  88.8 2.7 fusion.362
  91.9 2.7 fusion.362
  94.9 2.7 fusion.362
  97.9 2.7 fusion.362
  101.0 2.7 fusion.362
  104.0 2.7 fusion.362
  107.0 2.7 fusion.362
  110.0 2.7 fusion.362
  113.1 2.7 fusion.362
  116.1 2.7 fusion.362
  119.1 2.7 fusion.362
  122.1 2.7 fusion.362
  125.6 6.1 %add_bitcast_fusion = (f32[24,512,1,1]{1,2,3,0:T(1,128)S(1)}, f32[24,512,1]{1,2,0:T(1,128)S(1)}, f32[24,512,1]{1,2,0:T(1,128)S(1)}, f32[24,512,1]{1,2,0:T(1,128)...) fusion(f32[24,512,16]{1,2,0:T(8,128)S(1)} %get-tuple-element.24, ...), kind=kLoop, calls=%fused_computation.123 | loop fusion | flops 1155072 | bytes 4278464 | tf_op jit(solution)/shard_map/stack | solution.py:71
  132.9 1.3 stack.130
  150.8 2.0 stack.148
  152.9 3.0 stack.164
  157.1 1.2 constant_dynamic-update-slice_fusion.17
  158.3 2.1 constant_dynamic-update-slice_fusion.16
  160.3 2.0 constant_dynamic-update-slice_fusion.15
  163.4 1.2 constant_dynamic-update-slice_fusion.13
  164.6 2.1 constant_dynamic-update-slice_fusion.12
  166.7 1.3 constant_dynamic-update-slice_fusion.11
  169.1 1.2 constant_dynamic-update-slice_fusion.9
  170.3 1.3 constant_dynamic-update-slice_fusion.8
  171.6 1.3 constant_dynamic-update-slice_fusion.7
  174.0 1.2 constant_dynamic-update-slice_fusion.5
  175.2 1.3 constant_dynamic-update-slice_fusion.4
  176.6 1.4 constant_dynamic-update-slice_fusion.3
  179.0 1.2 constant_dynamic-update-slice_fusion.1
  180.2 1.2 constant_dynamic-update-slice_fusion
  183.0 1.2 fusion.36
  184.2 1.3 fusion.35
  185.4 1.4 subtract_dynamic-update-slice_fusion
  186.8 17.4 %copy.126 = f32[24,512,16,24]{1,3,2,0:T(8,128)S(1)} copy(f32[24,512,16,24]{1,2,3,0:T(8,128)} %subtract_dynamic-update-slice_fusion) | data formatting | bytes 37748736 | tf_op jit(solution)/shard_map/stack | solution.py:77
  204.4 6.3 %fusion.20 = bf16[24,512,384]{1,2,0:T(8,128)(2,1)} fusion(f32[24,512,16,24]{1,3,2,0:T(8,128)S(1)} %copy.126, f32[24]{0:T(128)S(1)} %copy-done.23, f32[512]{0:T(512)S(1)} %fusion.337, f32[24,384]{1,0:T(8,128)S(1)} %fusion.38), kind=kLoop, calls=%fused_computation.30 | loop fusion | flops 18874368 | bytes 28350560 | tf_op jit(solution)/shard_map/convert_element_type | solution.py:87
  210.6 7.9 %reshape.8824 = bf16[768,32,32]{2,1,0:T(8,128)(2,1)} reshape(bf16[16,2,24576]{2,1,0:T(2,128)(2,1)} %all-to-all-done) | data formatting | bytes 3145728
  218.5 9.5 %copy.129 = bf16[16,48,32,32]{2,0,3,1:T(8,128)(2,1)} copy(bf16[16,48,32,32]{3,2,1,0:T(8,128)(2,1)} %bitcast.85) | data formatting | bytes 3145728 | tf_op jit(solution)/shard_map/all_to_all | solution.py:121
  228.0 9.3 %reshape.8814 = bf16[24,2,512,32]{2,3,1,0:T(8,128)(2,1)} reshape(bf16[48,16,32,32]{2,1,3,0:T(8,128)(2,1)} %bitcast.86) | data formatting | bytes 3145728 | tf_op jit(solution)/shard_map/reshape | solution.py:128
  237.3 7.0 %fusion.352 = f32[24,384,64]{1,2,0:S(1)} fusion(bf16[24,512,384]{1,2,0:T(8,128)(2,1)} %fusion.20, bf16[24,512,64]{1,2,0:T(8,128)(2,1)} %bitcast.89), kind=kOutput, calls=%fused_computation.517 | convolution fusion | flops 603979776 | bytes 13369344
  245.5 1.6 all_to_all.28
  247.1 1.5 copy.132
  248.6 18.3 %all_to_all.34 = bf16[32,2,9216]{2,0,1:T(8,128)(2,1)S(1)} all-to-all(bf16[32,2,9216]{2,0,1:T(8,128)(2,1)S(1)} %copy.132), channel_id=1, replica_groups=mesh['lat'=16,'tm'=2] {'tm'}, dimensions={1} | all-to-all | bytes 2359296 | tf_op jit(solution)/shard_map/all_to_all | solution.py:135
  267.9 10.2 %reduce-scatter.2.cloned.1.call-done = f32[32,64]{1,0:T(8,128)} async-done(((f32[64,64]{1,0:T(8,128)}), f32[32,64]{1,0:T(8,128)}) %reduce-scatter.2.cloned.1.call-update) | async-done | bytes 8208 | tf_op jit(solution)/shard_map/reduce_scatter | solution.py:136
  278.1 60.6 %psum.14 = f32[32,64]{1,0:T(8,128)S(1)} all-reduce(f32[32,64]{1,0:T(8,128)} %reduce-scatter.2.cloned.1.call-done), channel_id=1, replica_groups=mesh['lat'=16,'tm'=2] {'lat'}, use_global_device_ids=true, to_apply=%region_3.4 | all-reduce | flops 2048 | bytes 16384 | tf_op jit(solution)/shard_map/psum | solution.py:144
  340.1 5.5 %psum.15 = f32[]{:T(128)} all-reduce(f32[]{:T(128)} %reduce_sum.9), channel_id=1, replica_groups=mesh['lat'=16,'tm'=2] {'tm'}, use_global_device_ids=true, to_apply=%region_5.6 | all-reduce | flops 1 | bytes 8 | tf_op jit(solution)/shard_map/psum | solution.py:146
  (298 shorter events, 39.0 us)
Async XLA Ops:
  6.5 1.6 copy-start
  44.7 165.9 %all-to-all-start = ((bf16[16,2,24576]{2,1,0:T(2,128)(2,1)}), bf16[16,2,24576]{2,1,0:T(2,128)(2,1)}, u32[]{:S(2)}, u32[]{:S(2)}) async-start(bf16[16,2,24576]{2,1,0:T(2,128)(2,1)} %reshape.8823), calls=%async_computation | async-start | bytes 3145728 | tf_op jit(solution)/shard_map/all_to_all | solution.py:121
  52.2 226.0 %reduce-scatter.2.cloned.1.call-start = ((), (), s32[]{:S(2)}) async-start(), calls=%async_computation.3 | async-start | bytes 49152 | tf_op jit(solution)/shard_map/reduce_scatter | solution.py:136
  52.4 82.7 %copy-start.21 = (f32[24]{0:T(128)}, f32[24]{0:T(128)S(1)}, u32[]{:S(2)}) copy-start(f32[24]{0:T(128)S(1)} %add_convert_fusion) | copy-start | bytes 292
  152.8 13.9 %copy-start.13 = (f32[24,16]{1,0:T(8,128)S(1)}, f32[24,16]{1,0:T(8,128)}, u32[]{:S(2)}) copy-start(f32[24,16]{1,0:T(8,128)} %copy.93) | copy-start | bytes 4612
  152.8 13.9 %copy-start.15 = (f32[24,16]{1,0:T(8,128)S(1)}, f32[24,16]{1,0:T(8,128)}, u32[]{:S(2)}) copy-start(f32[24,16]{1,0:T(8,128)} %copy.94) | copy-start | bytes 4612
  152.8 17.5 %copy-start.12 = (f32[24,16]{1,0:T(8,128)S(1)}, f32[24,16]{1,0:T(8,128)}, u32[]{:S(2)}) copy-start(f32[24,16]{1,0:T(8,128)} %copy.100) | copy-start | bytes 4612
  152.8 17.5 %copy-start.14 = (f32[24,16]{1,0:T(8,128)S(1)}, f32[24,16]{1,0:T(8,128)}, u32[]{:S(2)}) copy-start(f32[24,16]{1,0:T(8,128)} %copy.99) | copy-start | bytes 4612
  152.8 18.8 %copy-start.9 = (f32[24,16]{1,0:T(8,128)S(1)}, f32[24,16]{1,0:T(8,128)}, u32[]{:S(2)}) copy-start(f32[24,16]{1,0:T(8,128)} %copy.101) | copy-start | bytes 4612
  152.8 18.8 %copy-start.11 = (f32[24,16]{1,0:T(8,128)S(1)}, f32[24,16]{1,0:T(8,128)}, u32[]{:S(2)}) copy-start(f32[24,16]{1,0:T(8,128)} %copy.102) | copy-start | bytes 4612
  157.1 18.2 %copy-start.8 = (f32[24,16]{1,0:T(8,128)S(1)}, f32[24,16]{1,0:T(8,128)}, u32[]{:S(2)}) copy-start(f32[24,16]{1,0:T(8,128)} %copy.107) | copy-start | bytes 4612
  157.1 18.2 %copy-start.10 = (f32[24,16]{1,0:T(8,128)S(1)}, f32[24,16]{1,0:T(8,128)}, u32[]{:S(2)}) copy-start(f32[24,16]{1,0:T(8,128)} %copy.108) | copy-start | bytes 4612
  158.3 18.3 %copy-start.6 = (f32[24,16]{1,0:T(8,128)S(1)}, f32[24,16]{1,0:T(8,128)}, u32[]{:S(2)}) copy-start(f32[24,16]{1,0:T(8,128)} %copy.109) | copy-start | bytes 4612
  158.3 18.3 %copy-start.7 = (f32[24,16]{1,0:T(8,128)S(1)}, f32[24,16]{1,0:T(8,128)}, u32[]{:S(2)}) copy-start(f32[24,16]{1,0:T(8,128)} %copy.110) | copy-start | bytes 4612
  162.3 16.7 %copy-start.4 = (f32[24,16]{1,0:T(8,128)S(1)}, f32[24,16]{1,0:T(8,128)}, u32[]{:S(2)}) copy-start(f32[24,16]{1,0:T(8,128)} %copy.113) | copy-start | bytes 4612
  162.3 16.7 %copy-start.5 = (f32[24,16]{1,0:T(8,128)S(1)}, f32[24,16]{1,0:T(8,128)}, u32[]{:S(2)}) copy-start(f32[24,16]{1,0:T(8,128)} %copy.114) | copy-start | bytes 4612
  164.6 15.6 %copy-start.2 = (f32[24,16]{1,0:T(8,128)S(1)}, f32[24,16]{1,0:T(8,128)}, u32[]{:S(2)}) copy-start(f32[24,16]{1,0:T(8,128)} %copy.115) | copy-start | bytes 4612
  164.6 15.7 %copy-start.3 = (f32[24,16]{1,0:T(8,128)S(1)}, f32[24,16]{1,0:T(8,128)}, u32[]{:S(2)}) copy-start(f32[24,16]{1,0:T(8,128)} %copy.116) | copy-start | bytes 4612
  168.0 14.5 %copy-start.20 = (f32[24,16]{0,1:T(8,128)S(1)}, f32[24,16]{0,1:T(8,128)}, u32[]{:S(2)}) copy-start(f32[24,16]{0,1:T(8,128)} %get-tuple-element.404) | copy-start | bytes 4612
  168.0 14.6 %copy-start.19 = (f32[24,16]{0,1:T(8,128)S(1)}, f32[24,16]{0,1:T(8,128)}, u32[]{:S(2)}) copy-start(f32[24,16]{0,1:T(8,128)} %get-tuple-element.408) | copy-start | bytes 4612
  168.0 14.7 %copy-start.18 = (f32[24,16]{0,1:T(8,128)S(1)}, f32[24,16]{0,1:T(8,128)}, u32[]{:S(2)}) copy-start(f32[24,16]{0,1:T(8,128)} %get-tuple-element.405) | copy-start | bytes 4612
  168.0 14.7 %copy-start.17 = (f32[24,16]{0,1:T(8,128)S(1)}, f32[24,16]{0,1:T(8,128)}, u32[]{:S(2)}) copy-start(f32[24,16]{0,1:T(8,128)} %get-tuple-element.407) | copy-start | bytes 4612
  168.0 14.8 %copy-start.16 = (f32[24,16]{0,1:T(8,128)S(1)}, f32[24,16]{0,1:T(8,128)}, u32[]{:S(2)}) copy-start(f32[24,16]{0,1:T(8,128)} %get-tuple-element.383) | copy-start | bytes 4612
  186.8 17.5 %copy-start.22 = (f32[24]{0:T(128)S(1)}, f32[24]{0:T(128)}, u32[]{:S(2)}) copy-start(f32[24]{0:T(128)} %copy-done.21) | copy-start | bytes 292
  186.8 17.5 %copy-start.23 = (f32[24]{0:T(128)S(1)}, f32[24]{0:T(128)}, u32[]{:S(2)}) copy-start(f32[24]{0:T(128)} %get-tuple-element.429) | copy-start | bytes 292
  218.5 128.4 %copy-start.1 = (bf16[32,32,1024]{2,1,0:T(8,128)(2,1)S(1)}, bf16[32,32,1024]{2,1,0:T(8,128)(2,1)}, u32[]{:S(2)}) copy-start(bf16[32,32,1024]{2,1,0:T(8,128)(2,1)} %param.3) | copy-start | bytes 6291460
Sparse Core Ops, SparseCore 0:
  268.0 10.0 reduce-scatter.1
where the time goes:
time: 356 us; the launch traced here: 354 us
  other arithmetic  115 us (32%)
  local copies, waits for them, and re-layouts  96.8 us (27%)
  blocking collectives  84.4 us (24%)
  matrix products  24.4 us (7%)
  between operations  14.4 us (4%)
  waiting for transfers between devices  10.2 us (3%)
  starting transfers between devices  7.65 us (2%)
    sub x24, other arithmetic, compose(): diagonal_term * upper_right - mixed * lower_right  63.1 us
    psum x1, blocking collectives, local(): gram = lax.psum(partial_gram, 'lat')  60.6 us
    unnamed x24, other arithmetic  29 us
    unnamed x51, local copies, waits for them, and re-layouts  19.8 us
    all_to_all x1, blocking collectives, local(): lax.all_to_all(coefficients, 'tm', split_axis=1, concat_axis=0, tiled=True)  18.3 us
    another operation x1, local copies, waits for them, and re-layouts, legendre_blocks(): values = jnp.stack(outputs, axis=-1)  17.4 us
    dot_general x1, matrix products, local(): lax.dot_general(transform, flat_fields, (((1,), (1,)), ((), ())), preferr...  16.4 us
    reduce_scatter x1, waiting for transfers between devices, local(): lax.psum_scatter(lax.dot_general(columns, columns, (((1,), (1,)), ((), ()...  10.2 us
  transfers between devices with their start and end apart: 2, of which 1 were waited for; matrix products, arithmetic and copies ran while one was open for 45% of the time, Pallas kernels for 0%

commit v1 on v0

--- a/solution.py
+++ b/solution.py
@@ -141,7 +141,9 @@
         scatter_dimension=0,
         tiled=True,
     )
-    gram = lax.psum(partial_gram, "lat")
+    gram = partial_gram
+    for hop in (1, 2, 4, 8):
+        gram = gram + lax.ppermute(gram, "lat", [(dev, dev ^ hop) for dev in range(16)])
     own_block = lax.dynamic_slice_in_dim(gram, lax.axis_index("tm") * month_count, month_count, 1)
     trace_total = lax.psum(jnp.sum(jnp.diagonal(own_block)), "tm")
     return total_months * gram / (trace_total + 1e-06)

time: 356 us -> 311 us (0.87)
  blocking collectives: 84.4 us -> 23.8 us
  waiting for transfers between devices: 10.2 us -> 18.4 us
  starting transfers between devices: 7.65 us -> 13 us
    psum x1 -> x0, blocking collectives: 60.6 us -> none  [local(): gram = lax.psum(partial_gram, 'lat')]
    ppermute x0 -> x4, waiting for transfers between devices: none -> 8.17 us  [local(): lax.ppermute(gram, 'lat', [(dev, dev ^ hop) for dev in range(16)])]
    ppermute x0 -> x4, starting transfers between devices: none -> 5.33 us  [local(): lax.ppermute(gram, 'lat', [(dev, dev ^ hop) for dev in range(16)])]
  transfers between devices with their start and end apart: 2 -> 6, of which waited for: 1 -> 5; matrix products, arithmetic and copies ran while one was open for 45% -> 51% of each run, Pallas kernels for 0% -> 0%
where the time goes in v1:
time: 311 us; the launch traced here: 309 us
  other arithmetic  117 us (38%)
  local copies, waits for them, and re-layouts  96.9 us (31%)
  matrix products  24.5 us (8%)
  blocking collectives  23.8 us (8%)
  waiting for transfers between devices  18.4 us (6%)
  between operations  14.4 us (5%)
  starting transfers between devices  13 us (4%)
    sub x24, other arithmetic, compose(): diagonal_term * upper_right - mixed * lower_right  63.5 us
    unnamed x24, other arithmetic  29.5 us
    unnamed x51, local copies, waits for them, and re-layouts  19.9 us
    all_to_all x1, blocking collectives, local(): lax.all_to_all(coefficients, 'tm', split_axis=1, concat_axis=0, tiled=True)  18.3 us
    another operation x1, local copies, waits for them, and re-layouts, legendre_blocks(): values = jnp.stack(outputs, axis=-1)  17.4 us
    dot_general x1, matrix products, local(): lax.dot_general(transform, flat_fields, (((1,), (1,)), ((), ())), preferr...  16.4 us
    reduce_scatter x1, waiting for transfers between devices, local(): lax.psum_scatter(lax.dot_general(columns, columns, (((1,), (1,)), ((), ()...  10.2 us
    all_to_all x1, local copies, waits for them, and re-layouts, local(): lax.all_to_all(fourier, 'lat', split_axis=0, concat_axis=1, tiled=True)  9.49 us
  transfers between devices with their start and end apart: 6, of which 5 were waited for; matrix products, arithmetic and copies ran while one was open for 51% of the time, Pallas kernels for 0%

profile of v1, /device:TPU:0, one launch (start us, length us, event | category | flops | bytes accessed | tf_op | source)
XLA Modules:
  0.0 308.9 jit_solution(6018186835823905575)
XLA Ops:
  6.6 1.5 copy-done
  8.1 16.4 %convolution_convert_fusion = bf16[768,1024]{1,0:T(8,128)(2,1)} fusion(bf16[1024,1024]{1,0:T(8,128)(2,1)S(1)} %bitcast.84, f32[768]{0:T(1024)S(1)} %get-tuple-element.432, s32[768]{0:T(1024)S(1)} %fusion.324, pred[768]{0:T(1024)(128)(4,1)S(1)} %get-tuple-element.431), kind=kOutput, calls=%fused_computation.41 | convolution fusion | flops 1626341376 | bytes 3676928 | tf_op jit(solution)/shard_map/dot_general | solution.py:117
  24.5 1.7 copy.127
  26.2 9.2 %copy.128 = bf16[768,32,32]{2,1,0:T(8,128)(2,1)} copy(bf16[768,32,32]{0,2,1:T(8,128)(2,1)S(1)} %bitcast.90) | data formatting | bytes 3145728 | tf_op jit(solution)/shard_map/reshape | solution.py:120
  35.4 9.3 %reshape.8823 = bf16[16,2,24576]{2,1,0:T(2,128)(2,1)} reshape(bf16[768,32,32]{2,1,0:T(8,128)(2,1)} %copy.128) | data formatting | bytes 3145728
  44.8 7.4 %all-to-all-start = ((bf16[16,2,24576]{2,1,0:T(2,128)(2,1)}), bf16[16,2,24576]{2,1,0:T(2,128)(2,1)}, u32[]{:S(2)}, u32[]{:S(2)}) async-start(bf16[16,2,24576]{2,1,0:T(2,128)(2,1)} %reshape.8823), calls=%async_computation | async-start | bytes 3145728 | tf_op jit(solution)/shard_map/all_to_all | solution.py:121
  53.3 71.9 %while.25 = (s32[]{:T(128)}, f32[24,512,16]{1,2,0:T(8,128)S(1)}, f32[24,512,16]{1,2,0:T(8,128)}, f32[24,512,16]{1,2,0:T(8,128)S(1)}, f32[24,512,16]{1,2,0:T(8,128)S(1)}, /*index=5*/s32[]{:T(128)}, s32[]{:T(128)}, s32[]{:T(128)}) while((s32[]{:T(128)}, f32[24,512,16]{1,2,0:T(8,128)S(1)}, ...), condition=%wide.region_1.2_spmd.clone.clone.clone, body=%wide.region_0.1_spmd.clone.clone.clone.sunk | while | flops 1778076 | bytes 6308475 | solution.py:56
  53.7 1.6 fusion.362
  55.6 2.7 fusion.362
  58.6 2.7 fusion.362
  61.7 2.7 fusion.362
  64.7 2.7 fusion.362
  67.8 2.7 fusion.362
  70.8 2.7 fusion.362
  73.8 2.7 fusion.362
  76.9 2.7 fusion.362
  79.9 2.7 fusion.362
  83.0 2.7 fusion.362
  86.0 2.7 fusion.362
  89.1 2.7 fusion.362
  92.1 2.7 fusion.362
  95.1 2.7 fusion.362
  98.2 2.7 fusion.362
  101.2 2.7 fusion.362
  104.3 2.7 fusion.362
  107.3 2.7 fusion.362
  110.4 2.7 fusion.362
  113.4 2.7 fusion.362
  116.4 2.7 fusion.362
  119.5 2.7 fusion.362
  122.5 2.7 fusion.362
  126.0 6.5 %add_bitcast_fusion = (f32[24,512,1,1]{1,2,3,0:T(1,128)S(1)}, f32[24,512,1]{1,2,0:T(1,128)S(1)}, f32[24,512,1]{1,2,0:T(1,128)S(1)}, f32[24,512,1]{1,2,0:T(1,128)...) fusion(f32[24,512,16]{1,2,0:T(8,128)S(1)} %get-tuple-element.24, ...), kind=kLoop, calls=%fused_computation.123 | loop fusion | flops 1155072 | bytes 4278464 | tf_op jit(solution)/shard_map/stack | solution.py:71
  133.6 1.3 stack.130
  151.6 2.0 stack.148
  153.6 3.0 stack.164
  159.0 2.1 constant_dynamic-update-slice_fusion.16
  161.0 2.0 constant_dynamic-update-slice_fusion.15
  165.4 2.1 constant_dynamic-update-slice_fusion.12
  167.5 1.3 constant_dynamic-update-slice_fusion.11
  171.2 1.3 constant_dynamic-update-slice_fusion.8
  172.6 1.3 constant_dynamic-update-slice_fusion.7
  176.3 1.3 constant_dynamic-update-slice_fusion.4
  177.6 1.3 constant_dynamic-update-slice_fusion.3
  180.1 1.3 constant_dynamic-update-slice_fusion.1
  185.4 1.3 fusion.35
  186.7 1.4 subtract_dynamic-update-slice_fusion
  188.2 17.4 %copy.126 = f32[24,512,16,24]{1,3,2,0:T(8,128)S(1)} copy(f32[24,512,16,24]{1,2,3,0:T(8,128)} %subtract_dynamic-update-slice_fusion) | data formatting | bytes 37748736 | tf_op jit(solution)/shard_map/stack | solution.py:77
  205.7 6.3 %fusion.20 = bf16[24,512,384]{1,2,0:T(8,128)(2,1)} fusion(f32[24,512,16,24]{1,3,2,0:T(8,128)S(1)} %copy.126, f32[24]{0:T(128)S(1)} %copy-done.23, f32[512]{0:T(512)S(1)} %fusion.337, f32[24,384]{1,0:T(8,128)S(1)} %fusion.38), kind=kLoop, calls=%fused_computation.30 | loop fusion | flops 18874368 | bytes 28350560 | tf_op jit(solution)/shard_map/convert_element_type | solution.py:87
  212.0 7.9 %reshape.8824 = bf16[768,32,32]{2,1,0:T(8,128)(2,1)} reshape(bf16[16,2,24576]{2,1,0:T(2,128)(2,1)} %all-to-all-done) | data formatting | bytes 3145728
  219.9 9.5 %copy.129 = bf16[16,48,32,32]{2,0,3,1:T(8,128)(2,1)} copy(bf16[16,48,32,32]{3,2,1,0:T(8,128)(2,1)} %bitcast.85) | data formatting | bytes 3145728 | tf_op jit(solution)/shard_map/all_to_all | solution.py:121
  229.4 9.3 %reshape.8814 = bf16[24,2,512,32]{2,3,1,0:T(8,128)(2,1)} reshape(bf16[48,16,32,32]{2,1,3,0:T(8,128)(2,1)} %bitcast.86) | data formatting | bytes 3145728 | tf_op jit(solution)/shard_map/reshape | solution.py:128
  238.7 7.0 %fusion.352 = f32[24,384,64]{1,2,0:S(1)} fusion(bf16[24,512,384]{1,2,0:T(8,128)(2,1)} %fusion.20, bf16[24,512,64]{1,2,0:T(8,128)(2,1)} %bitcast.89), kind=kOutput, calls=%fused_computation.517 | convolution fusion | flops 603979776 | bytes 13369344
  246.9 1.6 all_to_all.28
  248.5 1.5 copy.132
  250.0 18.3 %all_to_all.34 = bf16[32,2,9216]{2,0,1:T(8,128)(2,1)S(1)} all-to-all(bf16[32,2,9216]{2,0,1:T(8,128)(2,1)S(1)} %copy.132), channel_id=1, replica_groups=mesh['lat'=16,'tm'=2] {'tm'}, dimensions={1} | all-to-all | bytes 2359296 | tf_op jit(solution)/shard_map/all_to_all | solution.py:135
  269.3 10.2 %reduce-scatter.2.cloned.1.call-done = f32[32,64]{1,0:T(8,128)} async-done(((f32[64,64]{1,0:T(8,128)}), f32[32,64]{1,0:T(8,128)}) %reduce-scatter.2.cloned.1.call-update) | async-done | bytes 8208 | tf_op jit(solution)/shard_map/reduce_scatter | solution.py:136
  279.6 1.4 collective-permute-done
  281.7 1.5 collective-permute-start.1
  283.1 2.3 collective-permute-done.1
  285.4 1.5 collective-permute-start.2
  286.9 2.3 collective-permute-done.2
  289.2 2.4 collective-permute-start.3
  291.6 2.2 collective-permute-done.3
  295.2 5.5 %psum.7 = f32[]{:T(128)} all-reduce(f32[]{:T(128)} %reduce_sum.9), channel_id=1, replica_groups=mesh['lat'=16,'tm'=2] {'tm'}, use_global_device_ids=true, to_apply=%region_4.5 | all-reduce | flops 1 | bytes 8 | tf_op jit(solution)/shard_map/psum | solution.py:148
  (309 shorter events, 47.3 us)
Async XLA Ops:
  6.5 1.6 copy-start
  44.8 167.3 %all-to-all-start = ((bf16[16,2,24576]{2,1,0:T(2,128)(2,1)}), bf16[16,2,24576]{2,1,0:T(2,128)(2,1)}, u32[]{:S(2)}, u32[]{:S(2)}) async-start(bf16[16,2,24576]{2,1,0:T(2,128)(2,1)} %reshape.8823), calls=%async_computation | async-start | bytes 3145728 | tf_op jit(solution)/shard_map/all_to_all | solution.py:121
  52.2 227.4 %reduce-scatter.2.cloned.1.call-start = ((), (), s32[]{:S(2)}) async-start(), calls=%async_computation.3 | async-start | bytes 49152 | tf_op jit(solution)/shard_map/reduce_scatter | solution.py:136
  52.5 83.5 %copy-start.21 = (f32[24]{0:T(128)}, f32[24]{0:T(128)S(1)}, u32[]{:S(2)}) copy-start(f32[24]{0:T(128)S(1)} %add_convert_fusion) | copy-start | bytes 292
  153.5 14.0 %copy-start.13 = (f32[24,16]{1,0:T(8,128)S(1)}, f32[24,16]{1,0:T(8,128)}, u32[]{:S(2)}) copy-start(f32[24,16]{1,0:T(8,128)} %copy.93) | copy-start | bytes 4612
  153.6 14.0 %copy-start.15 = (f32[24,16]{1,0:T(8,128)S(1)}, f32[24,16]{1,0:T(8,128)}, u32[]{:S(2)}) copy-start(f32[24,16]{1,0:T(8,128)} %copy.94) | copy-start | bytes 4612
  153.6 17.7 %copy-start.12 = (f32[24,16]{1,0:T(8,128)S(1)}, f32[24,16]{1,0:T(8,128)}, u32[]{:S(2)}) copy-start(f32[24,16]{1,0:T(8,128)} %copy.100) | copy-start | bytes 4612
  153.6 17.7 %copy-start.14 = (f32[24,16]{1,0:T(8,128)S(1)}, f32[24,16]{1,0:T(8,128)}, u32[]{:S(2)}) copy-start(f32[24,16]{1,0:T(8,128)} %copy.99) | copy-start | bytes 4612
  153.6 19.0 %copy-start.9 = (f32[24,16]{1,0:T(8,128)S(1)}, f32[24,16]{1,0:T(8,128)}, u32[]{:S(2)}) copy-start(f32[24,16]{1,0:T(8,128)} %copy.101) | copy-start | bytes 4612
  153.6 19.0 %copy-start.11 = (f32[24,16]{1,0:T(8,128)S(1)}, f32[24,16]{1,0:T(8,128)}, u32[]{:S(2)}) copy-start(f32[24,16]{1,0:T(8,128)} %copy.102) | copy-start | bytes 4612
  157.8 18.5 %copy-start.8 = (f32[24,16]{1,0:T(8,128)S(1)}, f32[24,16]{1,0:T(8,128)}, u32[]{:S(2)}) copy-start(f32[24,16]{1,0:T(8,128)} %copy.107) | copy-start | bytes 4612
  157.8 18.5 %copy-start.10 = (f32[24,16]{1,0:T(8,128)S(1)}, f32[24,16]{1,0:T(8,128)}, u32[]{:S(2)}) copy-start(f32[24,16]{1,0:T(8,128)} %copy.108) | copy-start | bytes 4612
  159.0 18.7 %copy-start.6 = (f32[24,16]{1,0:T(8,128)S(1)}, f32[24,16]{1,0:T(8,128)}, u32[]{:S(2)}) copy-start(f32[24,16]{1,0:T(8,128)} %copy.109) | copy-start | bytes 4612
  159.0 18.7 %copy-start.7 = (f32[24,16]{1,0:T(8,128)S(1)}, f32[24,16]{1,0:T(8,128)}, u32[]{:S(2)}) copy-start(f32[24,16]{1,0:T(8,128)} %copy.110) | copy-start | bytes 4612
  163.1 17.0 %copy-start.4 = (f32[24,16]{1,0:T(8,128)S(1)}, f32[24,16]{1,0:T(8,128)}, u32[]{:S(2)}) copy-start(f32[24,16]{1,0:T(8,128)} %copy.113) | copy-start | bytes 4612
  163.1 17.0 %copy-start.5 = (f32[24,16]{1,0:T(8,128)S(1)}, f32[24,16]{1,0:T(8,128)}, u32[]{:S(2)}) copy-start(f32[24,16]{1,0:T(8,128)} %copy.114) | copy-start | bytes 4612
  165.4 15.9 %copy-start.2 = (f32[24,16]{1,0:T(8,128)S(1)}, f32[24,16]{1,0:T(8,128)}, u32[]{:S(2)}) copy-start(f32[24,16]{1,0:T(8,128)} %copy.115) | copy-start | bytes 4612
  165.4 15.9 %copy-start.3 = (f32[24,16]{1,0:T(8,128)S(1)}, f32[24,16]{1,0:T(8,128)}, u32[]{:S(2)}) copy-start(f32[24,16]{1,0:T(8,128)} %copy.116) | copy-start | bytes 4612
  168.9 14.9 %copy-start.20 = (f32[24,16]{0,1:T(8,128)S(1)}, f32[24,16]{0,1:T(8,128)}, u32[]{:S(2)}) copy-start(f32[24,16]{0,1:T(8,128)} %get-tuple-element.404) | copy-start | bytes 4612
  168.9 14.9 %copy-start.19 = (f32[24,16]{0,1:T(8,128)S(1)}, f32[24,16]{0,1:T(8,128)}, u32[]{:S(2)}) copy-start(f32[24,16]{0,1:T(8,128)} %get-tuple-element.408) | copy-start | bytes 4612
  168.9 15.0 %copy-start.18 = (f32[24,16]{0,1:T(8,128)S(1)}, f32[24,16]{0,1:T(8,128)}, u32[]{:S(2)}) copy-start(f32[24,16]{0,1:T(8,128)} %get-tuple-element.405) | copy-start | bytes 4612
  168.9 15.1 %copy-start.17 = (f32[24,16]{0,1:T(8,128)S(1)}, f32[24,16]{0,1:T(8,128)}, u32[]{:S(2)}) copy-start(f32[24,16]{0,1:T(8,128)} %get-tuple-element.407) | copy-start | bytes 4612
  168.9 15.2 %copy-start.16 = (f32[24,16]{0,1:T(8,128)S(1)}, f32[24,16]{0,1:T(8,128)}, u32[]{:S(2)}) copy-start(f32[24,16]{0,1:T(8,128)} %get-tuple-element.383) | copy-start | bytes 4612
  188.2 17.5 %copy-start.22 = (f32[24]{0:T(128)S(1)}, f32[24]{0:T(128)}, u32[]{:S(2)}) copy-start(f32[24]{0:T(128)} %copy-done.21) | copy-start | bytes 292
  188.2 17.5 %copy-start.23 = (f32[24]{0:T(128)S(1)}, f32[24]{0:T(128)}, u32[]{:S(2)}) copy-start(f32[24]{0:T(128)} %get-tuple-element.429) | copy-start | bytes 292
  219.9 82.1 %copy-start.1 = (bf16[32,32,1024]{2,1,0:T(8,128)(2,1)S(1)}, bf16[32,32,1024]{2,1,0:T(8,128)(2,1)}, u32[]{:S(2)}) copy-start(bf16[32,32,1024]{2,1,0:T(8,128)(2,1)} %param.3) | copy-start | bytes 6291460
  279.6 1.4 collective-permute-start
  281.7 3.7 %collective-permute-start.1 = (f32[32,64]{1,0:T(8,128)S(1)}, f32[32,64]{1,0:T(8,128)S(1)}, u32[]{:S(2)}, u32[]{:S(2)}) collective-permute-start(f32[32,64]{1,0:T(8,128)S(1)} %add.2285), channel_id=1, source_target_pairs={{0,4},{2,6},{4,0},{6,2},{8,12},{10,14},{12,8},{14,10},{16,20},{18,... | collective-permute-start | bytes 24584 | tf_op jit(solution)/shard_map/ppermute | solution.py:146
  285.4 3.7 %collective-permute-start.2 = (f32[32,64]{1,0:T(8,128)S(1)}, f32[32,64]{1,0:T(8,128)S(1)}, u32[]{:S(2)}, u32[]{:S(2)}) collective-permute-start(f32[32,64]{1,0:T(8,128)S(1)} %add.2286), channel_id=1, source_target_pairs={{0,8},{2,10},{4,12},{6,14},{8,0},{10,2},{12,4},{14,6},{16,24},{18,... | collective-permute-start | bytes 24584 | tf_op jit(solution)/shard_map/ppermute | solution.py:146
  289.2 4.6 %collective-permute-start.3 = (f32[32,64]{1,0:T(8,128)S(1)}, f32[32,64]{1,0:T(8,128)S(1)}, u32[]{:S(2)}, u32[]{:S(2)}) collective-permute-start(f32[32,64]{1,0:T(8,128)S(1)} %add.2287), channel_id=1, source_target_pairs={{0,16},{2,18},{4,20},{6,22},{8,24},{10,26},{12,28},{14,30},{16,0},... | collective-permute-start | bytes 24584 | tf_op jit(solution)/shard_map/ppermute | solution.py:146
Sparse Core Ops, SparseCore 0:
  269.5 10.0 reduce-scatter.1
